TPU v7x, 32 devices: a whole 2x2x4 slice. The times are simulated.
32 devices in a mesh: cell: 2 (over x), seq: 16 (over z, y, core).
Axes of the slice: x: 2, y: 2, z: 4, core: 2. Of those that a mesh axis runs over, the one named last changes fastest.
Arguments:
- queries: bfloat16 [128, 6144], P(('cell', 'seq')), parts along dimension 0, may hold values from -500 to 500
- keys: bfloat16 [256, 128, 1024], P(('cell', 'seq')), parts along dimension 0, may hold values from -6 to 6
- values: bfloat16 [256, 128, 1024], P(('cell', 'seq')), parts along dimension 0, may hold values from -6 to 6
- page_request: int32 [256], P(('cell', 'seq')), parts along dimension 0, may hold values from 0 to 63, as said below
- page_fill: int32 [256], P(('cell', 'seq')), parts along dimension 0, may hold values from 0 to 128
Outputs:
- attended: bfloat16 [128, 6144], P(('cell', 'seq')), parts along dimension 0
There are 2 independent parts, one for each index of `cell`. A program takes and returns all parts, laid end to end along the dimension named above; each array names one. Nothing has to cross between parts.
Inputs may be any that keep to these rules, and one draw needn't show every extreme that they name: `page_request`: every request has at least one page with a live slot. Request r's home is index r // 4 of seq; among one device's pages, the requests of any one home are at most 2 distinct ones, and some device reaches that.
All inputs are finite; a program needn't handle non-finite values.
Results may differ from a plain program's by a relative error of at most 0.0035.
Values may be sent and summed in bfloat16 or wider, within the bound.
No kernel may reach another device: no remote copies, remote signals or barrier semaphores. Data moves between devices by JAX's collectives and lax.ppermute only.
A program may use at most 64 MiB of HBM per device.

v0:
```python
import functools

import jax
import jax.numpy as jnp
from jax import lax
from jax.experimental import pallas as pl
from jax.experimental.pallas import tpu as pltpu
from jax.sharding import PartitionSpec as P


HEADS = 48
KV_HEADS = 8
HEAD_DIM = 128
GROUP = 6
LANES = 128
HALF = LANES // 2

FLOOR = -30000.0
LAYER = 4
STAGE_FLOPS = 20_000_000_000


def exchange(x, step, count):
    return lax.ppermute(x, "seq", [(i, i ^ step) for i in range(count)])


def gather_queries(queries, count):
    far = [4 * k for k in range(count // 4 - 1, 0, -1)]
    pieces = {0: queries}
    for step in far:
        pieces[step] = exchange(queries, step, count)
    for step in [0] + far[::-1]:
        pieces[step ^ 2] = exchange(pieces[step], 2, count)
    for step in list(pieces):
        pieces[step ^ 1] = exchange(pieces[step], 1, count)
    return [pieces[k] for k in range(count)]


def spread_out(block, rows, put):
    req_dev = block.shape[0]
    block = block[...].astype(jnp.float32)
    for h in range(HEADS):
        rows[req_dev * h : req_dev * (h + 1), :] = block[:, LANES * h : LANES * (h + 1)]
    for r in range(req_dev):
        put(r, rows[pl.ds(r, HEADS, stride=req_dev), :].astype(jnp.bfloat16))


def stage_kernel(*refs):
    blocks, (held, rows) = refs[:-2], refs[-2:]
    for k, block in enumerate(blocks):

        def put(r, tile, k=k):
            held[k, r] = tile

        spread_out(block, rows.at[k], put)


def stage(blocks):
    spec = pl.BlockSpec(memory_space=pltpu.VMEM)
    req_dev = blocks[0].shape[0]
    return pl.pallas_call(
        stage_kernel,
        name="stage",
        out_shape=jax.ShapeDtypeStruct((len(blocks), req_dev, HEADS, HEAD_DIM), jnp.bfloat16),
        in_specs=[spec] * len(blocks),
        out_specs=spec,
        scratch_shapes=[pltpu.VMEM((len(blocks), HEADS * req_dev, LANES), jnp.float32)],
        compiler_params=pltpu.CompilerParams(vmem_limit_bytes=16 * 2**20),
        cost_estimate=pl.CostEstimate(flops=STAGE_FLOPS, bytes_accessed=0, transcendentals=0),
    )(*blocks)


def split3(x):
    high = x.astype(jnp.bfloat16).astype(jnp.float32)
    middle = (x - high).astype(jnp.bfloat16).astype(jnp.float32)
    low = (x - high - middle).astype(jnp.bfloat16).astype(jnp.float32)
    return [high, middle, low]


def scalars(x):
    return [x[0, i] for i in range(x.shape[1])]


def divide(x, by):
    return x >> by.bit_length() - 1 if by & (by - 1) == 0 else x // by


def remainder(x, by):
    return x & (by - 1) if by & (by - 1) == 0 else x % by


def attend_kernel(late, by_xor, request_ref, fill_ref, held, *refs):
    late_refs, (keys, values, send, tail, rows, accs) = refs[:late], refs[late:]
    pages, page_len, _ = keys.shape
    early, req_dev, _, _ = held.shape
    me = lax.axis_index("seq") if by_xor else 0
    where = request_ref[...]
    block_at = divide(where, req_dev)
    if by_xor:
        block_at = remainder((block_at ^ me) + early + late - 1, early + late)
    block_at = scalars(block_at)
    row_at = scalars(remainder(where, req_dev))
    fill = scalars(fill_ref[...])
    for k in range(late):

        def put(r, tile, k=k):
            tail[k, r] = tile

        spread_out(late_refs[k], rows.at[k], put)
    lane = lax.broadcasted_iota(jnp.int32, (HEADS, LANES), 1)
    kv_of = lax.broadcasted_iota(jnp.int32, (HEADS, LANES), 0) // GROUP

    for p in range(pages):
        query = held[jnp.minimum(block_at[p], early - 1), row_at[p]]
        if late:
            last = tail[jnp.maximum(block_at[p] - early, 0), row_at[p]]
            query = jnp.where(block_at[p] < early, query, last)
        zero = jnp.zeros_like(query)
        wide = jnp.concatenate([jnp.where(kv_of == k, query, zero) for k in range(KV_HEADS)], axis=1)
        accs[p] = lax.dot_general(
            wide, keys[p], (((1,), (1,)), ((), ())), preferred_element_type=jnp.float32
        ) * HEAD_DIM ** (-0.5)

    heavy, totals = [], []
    stats = jnp.zeros((HEADS, LANES), jnp.float32)
    for p in range(pages):
        scores = accs[p]
        live = lax.broadcasted_iota(jnp.int32, (HEADS, page_len), 1) < fill[p]
        peak = jnp.max(jnp.where(live, scores, FLOOR), axis=1, keepdims=True)
        weights = jnp.where(live, jnp.exp(scores - peak), 0.0).astype(jnp.bfloat16)
        total = jnp.sum(weights.astype(jnp.float32), axis=1, keepdims=True)
        heavy.append(weights)
        totals.append(total)
        stats = jnp.where(lane == p, peak, stats)
        stats = jnp.where(lane == pages + p, total, stats)
    high, middle, low = split3(stats)
    stats = high + pltpu.roll(middle, 2 * pages, 1) + pltpu.roll(low, 4 * pages, 1)
    index = [divide(where, req_dev), remainder(where, req_dev)]
    index = jnp.concatenate(index + [jnp.zeros((1, LANES - 2 * pages), jnp.int32)], axis=1)
    index = pltpu.roll(index.astype(jnp.float32), 6 * pages, 1)
    inside = jnp.logical_and(lane >= 6 * pages, lane < 8 * pages)
    send[HEADS * pages :, :] = jnp.where(inside, index, stats).astype(send.dtype)

    for p in range(pages):
        mixed = lax.dot_general(
            heavy[p], values[p], (((1,), (0,)), ((), ())), preferred_element_type=jnp.float32
        )
        acc = mixed[:, :LANES]
        for k in range(1, KV_HEADS):
            acc = jnp.where(kv_of == k, mixed[:, LANES * k : LANES * (k + 1)], acc)
        send[HEADS * p : HEADS * (p + 1), :] = (acc / jnp.maximum(totals[p], 1.0)).astype(send.dtype)


def attend(held, late, by_xor, keys, values, page_request, page_fill):
    pages = keys.shape[0]
    req_dev = held.shape[1]
    vmem = pl.BlockSpec(memory_space=pltpu.VMEM)
    return pl.pallas_call(
        functools.partial(attend_kernel, len(late), by_xor),
        name="attend",
        out_shape=jax.ShapeDtypeStruct(((pages + 1) * HEADS, LANES), jnp.bfloat16),
        in_specs=[vmem] * (len(late) + 5),
        out_specs=vmem,
        scratch_shapes=[
            pltpu.VMEM((max(len(late), 1), req_dev, HEADS, HEAD_DIM), jnp.bfloat16),
            pltpu.VMEM((max(len(late), 1), HEADS * req_dev, LANES), jnp.float32),
            pltpu.VMEM((pages, HEADS, HEAD_DIM), jnp.float32),
        ],
        compiler_params=pltpu.CompilerParams(vmem_limit_bytes=32 * 2**20),
    )(page_request, page_fill, held, *late, keys, values)


def page_tables(blocks, slots, req_dev):
    pages = blocks[0].shape[0] // HEADS - 1
    me = lax.axis_index("seq")
    lane = lax.broadcasted_iota(jnp.int32, (HEADS, LANES), 1)
    peaks = jnp.full((HEADS, LANES), FLOOR, jnp.float32)
    totals = jnp.zeros((HEADS, LANES), jnp.float32)
    home = jnp.full((1, LANES), -1.0, jnp.float32)
    local = jnp.zeros((1, LANES), jnp.float32)
    for s, block in enumerate(blocks):
        stats = block[HEADS * pages :, :].astype(jnp.float32)
        whole = stats + pltpu.roll(stats, LANES - 2 * pages, 1) + pltpu.roll(stats, LANES - 4 * pages, 1)
        inside = jnp.logical_and(lane >= pages * s, lane < pages * (s + 1))
        peaks = jnp.where(inside, pltpu.roll(whole, (pages * s) % LANES, 1), peaks)
        totals = jnp.where(inside, pltpu.roll(whole, (pages * (s - 1)) % LANES, 1), totals)
        home = jnp.where(inside[:1], pltpu.roll(stats[:1], (pages * (s - 6)) % LANES, 1), home)
        local = jnp.where(inside[:1], pltpu.roll(stats[:1], (pages * (s - 7)) % LANES, 1), local)
    apart = home.astype(jnp.int32) ^ me
    mine = jnp.logical_and(home >= 0.0, remainder(apart, LAYER) == 0)
    where = jnp.where(mine, divide(apart, LAYER) * req_dev + local.astype(jnp.int32), slots)
    return peaks, totals, where


def layer_kernel(req_dev, *refs):
    blocks, outs, (sums, place, index, sem) = refs[:LAYER], refs[LAYER:-4], refs[-4:]
    pages = blocks[0].shape[0] // HEADS - 1
    slots = sums.shape[0] - 1
    lane = lax.broadcasted_iota(jnp.int32, (HEADS, LANES), 1)
    peaks, totals, where = page_tables(blocks, slots, req_dev)
    place[...] = where
    copy = pltpu.make_async_copy(place, index, sem)
    copy.start()
    sums[...] = jnp.zeros_like(sums)
    tops = jnp.zeros((HEADS, LANES), jnp.float32)
    slot_tops = jnp.full((HEADS, LANES), FLOOR, jnp.float32)
    for k in range(slots):
        top = jnp.max(jnp.where(where == k, peaks, FLOOR), axis=1, keepdims=True)
        tops = jnp.where(where == k, top, tops)
        slot_tops = jnp.where(lane == k, top, slot_tops)
    shares = jnp.where(where < slots, totals * jnp.exp(peaks - tops), 0.0)
    norms = jnp.ones((HEADS, LANES), jnp.float32)
    slot_wholes = jnp.zeros((HEADS, LANES), jnp.float32)
    for k in range(slots):
        whole = jnp.sum(jnp.where(where == k, shares, 0.0), axis=1, keepdims=True)
        slot_wholes = jnp.where(lane == k, whole, slot_wholes)
        norms = jnp.where(where == k, whole, norms)
    shares = shares / jnp.maximum(norms, 1.0)
    copy.wait()
    for i in range(LAYER * pages):
        s, p = divmod(i, pages)
        row = blocks[s][HEADS * p : HEADS * (p + 1), :].astype(jnp.float32)
        sums[index[0, i]] += row * shares[:, i : i + 1]

    pad = jnp.zeros((LANES - HEADS, LANES), jnp.float32)
    parts = []
    for table in (slot_tops, slot_wholes):
        flat = jnp.transpose(jnp.concatenate([table, pad], axis=0))
        parts += split3(flat[:slots])
    for k in range(len(outs)):
        for r in range(req_dev):
            outs[k][HEADS * r : HEADS * (r + 1), :] = sums[req_dev * k + r].astype(outs[k].dtype)
        lines = []
        for part in parts:
            part = part[req_dev * k : req_dev * (k + 1)]
            part = jnp.concatenate([part, jnp.zeros((8 - req_dev, LANES), jnp.float32)], axis=0)
            lines.append(part + pltpu.roll(pltpu.roll(part, 8 - req_dev // 2, 0), HALF, 1))
        tail = [line[: req_dev // 2] for line in lines]
        spare = outs[k].shape[0] - HEADS * req_dev - 3 * req_dev
        if spare:
            tail.append(jnp.zeros((spare, LANES), jnp.float32))
        outs[k][HEADS * req_dev :, :] = jnp.concatenate(tail, axis=0).astype(outs[k].dtype)


def layer_merge(own, count, homes, req_dev):
    vmem = pl.BlockSpec(memory_space=pltpu.VMEM)
    across = exchange(own, 2, count)
    blocks = [own, exchange(own, 1, count), across, exchange(across, 1, count)]
    height = HEADS * req_dev + -(-3 * req_dev // 8) * 8
    return pl.pallas_call(
        functools.partial(layer_kernel, req_dev),
        name="layer_merge",
        out_shape=[jax.ShapeDtypeStruct((height, LANES), jnp.bfloat16)] * homes,
        in_specs=[vmem] * LAYER,
        out_specs=[vmem] * homes,
        scratch_shapes=[
            pltpu.VMEM((homes * req_dev + 1, HEADS, HEAD_DIM), jnp.float32),
            pltpu.VMEM((1, LANES), jnp.int32),
            pltpu.SMEM((1, LANES), jnp.int32),
            pltpu.SemaphoreType.DMA,
        ],
        compiler_params=pltpu.CompilerParams(vmem_limit_bytes=16 * 2**20),
    )(*blocks)


def home_kernel(*refs):
    blocks, (out, accs) = refs[:-2], refs[-2:]
    req_dev = out.shape[0]
    half = req_dev // 2
    start = HEADS * req_dev
    peaks, totals = [], []
    for block in blocks:
        stats = block[start:, :].astype(jnp.float32)
        lines = [stats[half * i : half * (i + 1)] for i in range(6)]
        peaks.append(lines[0] + lines[1] + lines[2])
        totals.append(lines[3] + lines[4] + lines[5])
    top = functools.reduce(jnp.maximum, peaks)
    shares = [total * jnp.exp(peak - top) for peak, total in zip(peaks, totals)]
    whole = functools.reduce(jnp.add, shares)
    lane = lax.broadcasted_iota(jnp.int32, whole.shape, 1)
    whole = jnp.where(lane % HALF < HEADS, whole, 1.0)
    weights = [share / whole for share in shares]
    used = half * len(blocks)
    pad = jnp.zeros((LANES - used, LANES), jnp.float32)
    turned = jnp.transpose(jnp.concatenate(weights + [pad], axis=0))
    for r in range(req_dev):
        base = HALF * (r // half)
        acc = jnp.zeros((HEADS, HEAD_DIM), jnp.float32)
        for b, block in enumerate(blocks):
            column = half * b + r % half
            weight = turned[base : base + HEADS, column : column + 1]
            acc = acc + block[HEADS * r : HEADS * (r + 1), :].astype(jnp.float32) * weight
        accs[HEADS * r : HEADS * (r + 1), :] = acc
    for h in range(HEADS):
        out[:, LANES * h : LANES * (h + 1)] = accs[pl.ds(h, req_dev, stride=HEADS), :].astype(out.dtype)


def home_merge(blocks, req_dev):
    vmem = pl.BlockSpec(memory_space=pltpu.VMEM)
    return pl.pallas_call(
        home_kernel,
        name="home_merge",
        out_shape=jax.ShapeDtypeStruct((req_dev, HEADS * HEAD_DIM), jnp.bfloat16),
        in_specs=[vmem] * len(blocks),
        out_specs=vmem,
        scratch_shapes=[pltpu.VMEM((req_dev * HEADS, HEAD_DIM), jnp.float32)],
        compiler_params=pltpu.CompilerParams(vmem_limit_bytes=16 * 2**20),
    )(*blocks)


def steps(queries, keys, values, page_request, page_fill):
    count = lax.axis_size("seq")
    req_dev = queries.shape[0]
    page_request, page_fill = page_request[None], page_fill[None]
    by_xor = count <= 16
    if by_xor:
        pieces, late = gather_queries(queries, count), 3
        pieces = pieces[1:] + pieces[:1]
    else:
        whole, late = lax.all_gather(queries, "seq", axis=0), 0
        pieces = [whole[k] for k in range(count)]
    early = count - late
    own = attend(stage(pieces[:early]), pieces[early:], by_xor, keys, values, page_request, page_fill)
    blocks = list(layer_merge(own, count, count // LAYER, req_dev))
    order = [k for k in range(count // LAYER - 1, 0, -1)]
    if len(order) == 3:
        order = [2, 3, 1]
    far = [exchange(blocks[k], LAYER * k, count) for k in order]
    return home_merge(blocks[:1] + far, req_dev)


def solution(mesh):
    placed = (
        P(("cell", "seq"), None),
        P(("cell", "seq"), None, None),
        P(("cell", "seq"), None, None),
        P(("cell", "seq")),
        P(("cell", "seq")),
    )
    return jax.shard_map(steps, mesh=mesh, in_specs=placed, out_specs=P(("cell", "seq"), None), check_vma=False)
```

profile of v0, /device:TPU:0, one launch (start us, length us, event | category | flops | bytes accessed | tf_op | source)
XLA Modules:
  0.0 36.0 jit_solution(2040803961444726372)
XLA Ops:
  0.0 4.1 %collective-permute-start.7 = (bf16[4,6144]{1,0:T(4,128)(2,1)}, bf16[4,6144]{1,0:T(4,128)(2,1)S(1)}, u32[]{:S(2)}, u32[]{:S(2)}) collective-permute-start(bf16[4,6144]{1,0:T(4,128)(2,1)} %refs_2_.1), channel_id=1, source_target_pairs={{0,8},{1,9},{2,10},{3,11},{4,12},{5,13},{6,14},{7,15},{8,0},{9,1},... | collective-permute-start | bytes 147464 | tf_op jit(solution)/shard_map/ppermute | solution.py:24
  4.2 1.6 %collective-permute-start.3 = (bf16[4,6144]{1,0:T(4,128)(2,1)}, bf16[4,6144]{1,0:T(4,128)(2,1)S(1)}, u32[]{:S(2)}, u32[]{:S(2)}) collective-permute-start(bf16[4,6144]{1,0:T(4,128)(2,1)} %refs_2_.1), channel_id=1, source_target_pairs={{0,4},{1,5},{2,6},{3,7},{4,0},{5,1},{6,2},{7,3},{8,12},{9,13},{10,... | collective-permute-start | bytes 147464 | tf_op jit(solution)/shard_map/ppermute | solution.py:24
  5.7 0.0 collective-permute-start.11
  5.7 1.7 %collective-permute-start.1 = (bf16[4,6144]{1,0:T(4,128)(2,1)}, bf16[4,6144]{1,0:T(4,128)(2,1)S(1)}, u32[]{:S(2)}, u32[]{:S(2)}) collective-permute-start(bf16[4,6144]{1,0:T(4,128)(2,1)} %refs_2_.1), channel_id=1, source_target_pairs={{0,2},{1,3},{2,0},{3,1},{4,6},{5,7},{6,4},{7,5},{8,10},{9,11},{10,... | collective-permute-start | bytes 147464 | tf_op jit(solution)/shard_map/ppermute | solution.py:24
  7.5 0.0 collective-permute-start
  7.5 0.0 collective-permute-done.7.refs_7_
  7.5 1.3 %collective-permute-start.9 = (bf16[4,6144]{1,0:T(4,128)(2,1)S(1)}, bf16[4,6144]{1,0:T(4,128)(2,1)S(1)}, u32[]{:S(2)}, u32[]{:S(2)}) collective-permute-start(bf16[4,6144]{1,0:T(4,128)(2,1)S(1)} %collective-permute-done.7.refs_7_), channel_id=1, source_target_pairs={{0,2},{1,3},{2,0},{3,1},{4,6},{5,7},{6,4},{7,5},{8,10},{9,11},{10,... | collective-permute-start | bytes 147464 | tf_op jit(solution)/shard_map/ppermute | solution.py:24
  8.8 0.0 collective-permute-done.3.refs_3_
  8.8 1.2 %collective-permute-start.5 = (bf16[4,6144]{1,0:T(4,128)(2,1)S(1)}, bf16[4,6144]{1,0:T(4,128)(2,1)S(1)}, u32[]{:S(2)}, u32[]{:S(2)}) collective-permute-start(bf16[4,6144]{1,0:T(4,128)(2,1)S(1)} %collective-permute-done.3.refs_3_), channel_id=1, source_target_pairs={{0,2},{1,3},{2,0},{3,1},{4,6},{5,7},{6,4},{7,5},{8,10},{9,11},{10,... | collective-permute-start | bytes 147464 | tf_op jit(solution)/shard_map/ppermute | solution.py:24
  10.0 1.9 %collective-permute-done.11.refs_11_ = bf16[4,6144]{1,0:T(4,128)(2,1)S(1)} collective-permute-done((bf16[4,6144]{1,0:T(4,128)(2,1)}, bf16[4,6144]{1,0:T(4,128)(2,1)S(1)}, u32[]{:S(2)}, u32[]{:S(2)}) %collective-permute-start.11) | collective-permute-done | bytes 49184 | tf_op jit(solution)/shard_map/ppermute | solution.py:24
  11.8 0.0 collective-permute-start.12
  11.8 0.0 collective-permute-done.1.refs_1_
  11.8 0.5 %collective-permute-start.4 = (bf16[4,6144]{1,0:T(4,128)(2,1)S(1)}, bf16[4,6144]{1,0:T(4,128)(2,1)S(1)}, u32[]{:S(2)}, u32[]{:S(2)}) collective-permute-start(bf16[4,6144]{1,0:T(4,128)(2,1)S(1)} %collective-permute-done.3.refs_3_), channel_id=1, source_target_pairs={{0,1},{1,0},{2,3},{3,2},{4,5},{5,4},{6,7},{7,6},{8,9},{9,8},{10,11... | collective-permute-start | bytes 147464 | tf_op jit(solution)/shard_map/ppermute | solution.py:24
  12.4 0.0 collective-permute-done.refs_0_
  12.4 0.1 collective-permute-start.8
  12.4 0.0 collective-permute-done.9.refs_9_
  12.4 1.5 %collective-permute-start.13 = (bf16[4,6144]{1,0:T(4,128)(2,1)S(1)}, bf16[4,6144]{1,0:T(4,128)(2,1)S(1)}, u32[]{:S(2)}, u32[]{:S(2)}) collective-permute-start(bf16[4,6144]{1,0:T(4,128)(2,1)S(1)} %collective-permute-done.11.refs_11_), channel_id=1, source_target_pairs={{0,2},{1,3},{2,0},{3,1},{4,6},{5,7},{6,4},{7,5},{8,10},{9,11},{10,... | collective-permute-start | bytes 147464 | tf_op jit(solution)/shard_map/ppermute | solution.py:24
  13.9 0.0 collective-permute-done.5.refs_5_
  14.0 0.2 collective-permute-start.2
  14.1 0.0 collective-permute-done.12.refs_12_
  14.1 0.3 collective-permute-start.10
  14.5 0.0 collective-permute-done.4.refs_4_
  14.5 0.2 collective-permute-start.6
  14.6 1.9 %collective-permute-done.13.refs_0_ = bf16[4,6144]{1,0:T(4,128)(2,1)S(1)} collective-permute-done((bf16[4,6144]{1,0:T(4,128)(2,1)S(1)}, bf16[4,6144]{1,0:T(4,128)(2,1)S(1)}, u32[]{:S(2)}, u32[]{:S(2)}) %collective-permute-start.13) | collective-permute-done | bytes 49184 | tf_op jit(solution)/shard_map/ppermute | solution.py:24
  16.5 0.0 collective-permute-start.14
  16.5 0.0 collective-permute-done.8.refs_8_
  16.5 0.0 collective-permute-done.2.refs_2_
  16.5 0.0 collective-permute-done.10.refs_10_
  16.5 0.0 collective-permute-done.6.refs_6_
  16.6 0.3 stage.1.held
  16.8 0.9 %collective-permute-done.14.refs_1_ = bf16[4,6144]{1,0:T(4,128)(2,1)S(1)} collective-permute-done((bf16[4,6144]{1,0:T(4,128)(2,1)S(1)}, bf16[4,6144]{1,0:T(4,128)(2,1)S(1)}, u32[]{:S(2)}, u32[]{:S(2)}) %collective-permute-start.14) | collective-permute-done | bytes 49184 | tf_op jit(solution)/shard_map/ppermute | solution.py:24
  17.8 0.0 copy-done.4
  17.8 0.0 copy-done
  17.8 1.2 %attend.1.refs_0_ = bf16[432,128]{1,0:T(8,128)(2,1)S(1)} custom-call(s32[1,8]{1,0:T(1,128)S(1)} %bitcast.2, s32[1,8]{1,0:T(1,128)S(1)} %bitcast.3, bf16[13,4,48,128]{3,2,1,0:T(8,128)(2,1)S(1)} %stage.1.held, bf16[4,6144]{1,0:T(4,128)(2,1)S(1)} %collective-permute-done.13.refs_0_, bf16[4,6144]{1,0:T(4,128)(2,1)S(1)} %collective-permute-done.14.refs_1_, ...), custom_call_target="tpu_custom_call" | custom-call | tf_op jit(solution)/shard_map/attend/pallas_call | solution.py:158
  19.0 1.6 %collective-permute-start.16 = (bf16[432,128]{1,0:T(8,128)(2,1)S(1)}, bf16[432,128]{1,0:T(8,128)(2,1)S(1)}, u32[]{:S(2)}, u32[]{:S(2)}) collective-permute-start(bf16[432,128]{1,0:T(8,128)(2,1)S(1)} %attend.1.refs_0_), channel_id=1, source_target_pairs={{0,2},{1,3},{2,0},{3,1},{4,6},{5,7},{6,4},{7,5},{8,10},{9,11},{10,... | collective-permute-start | bytes 331784 | tf_op jit(solution)/shard_map/ppermute | solution.py:24
  20.6 0.0 collective-permute-start.15
  20.6 3.6 %collective-permute-done.16.refs_2_ = bf16[432,128]{1,0:T(8,128)(2,1)S(1)} collective-permute-done((bf16[432,128]{1,0:T(8,128)(2,1)S(1)}, bf16[432,128]{1,0:T(8,128)(2,1)S(1)}, u32[]{:S(2)}, u32[]{:S(2)}) %collective-permute-start.16) | collective-permute-done | bytes 110624 | tf_op jit(solution)/shard_map/ppermute | solution.py:24
  24.2 0.0 collective-permute-start.17
  24.2 0.0 collective-permute-done.15.refs_1_
  24.2 1.3 %collective-permute-done.17.refs_3_ = bf16[432,128]{1,0:T(8,128)(2,1)S(1)} collective-permute-done((bf16[432,128]{1,0:T(8,128)(2,1)S(1)}, bf16[432,128]{1,0:T(8,128)(2,1)S(1)}, u32[]{:S(2)}, u32[]{:S(2)}) %collective-permute-start.17) | collective-permute-done | bytes 110624 | tf_op jit(solution)/shard_map/ppermute | solution.py:24
  25.5 1.1 %layer_merge.1 = (bf16[208,128]{1,0:T(8,128)(2,1)S(1)}, bf16[208,128]{1,0:T(8,128)(2,1)S(1)}, bf16[208,128]{1,0:T(8,128)(2,1)S(1)}, bf16[208,128]{1,0:T(8,128)(2,1)S(1)}) custom-call(bf16[432,128]{1,0:T(8,128)(2,1)S(1)} %attend.1.refs_0_, bf16[432,128]{1,0:T(8,128)(2,1)S(1)} %collective-permute-done.15.refs_1_, ...), custom_call_target="tpu_custom_call" | custom-call | tf_op jit(solution)/shard_map/layer_merge/pallas_call | solution.py:250
  26.6 1.5 %collective-permute-start.18 = (bf16[208,128]{1,0:T(8,128)(2,1)S(1)}, bf16[208,128]{1,0:T(8,128)(2,1)S(1)}, u32[]{:S(2)}, u32[]{:S(2)}) collective-permute-start(bf16[208,128]{1,0:T(8,128)(2,1)S(1)} %get-tuple-element.10), channel_id=1, source_target_pairs={{0,8},{1,9},{2,10},{3,11},{4,12},{5,13},{6,14},{7,15},{8,0},{9,1},... | collective-permute-start | bytes 159752 | tf_op jit(solution)/shard_map/ppermute | solution.py:24
  28.0 2.1 %collective-permute-start.19 = (bf16[208,128]{1,0:T(8,128)(2,1)S(1)}, bf16[208,128]{1,0:T(8,128)(2,1)S(1)}, u32[]{:S(2)}, u32[]{:S(2)}) collective-permute-start(bf16[208,128]{1,0:T(8,128)(2,1)S(1)} %get-tuple-element.11), channel_id=1, source_target_pairs={{0,12},{1,13},{2,14},{3,15},{4,8},{5,9},{6,10},{7,11},{8,4},{9,5},... | collective-permute-start | bytes 159752 | tf_op jit(solution)/shard_map/ppermute | solution.py:24
  30.1 0.5 %collective-permute-start.20 = (bf16[208,128]{1,0:T(8,128)(2,1)S(1)}, bf16[208,128]{1,0:T(8,128)(2,1)S(1)}, u32[]{:S(2)}, u32[]{:S(2)}) collective-permute-start(bf16[208,128]{1,0:T(8,128)(2,1)S(1)} %get-tuple-element.12), channel_id=1, source_target_pairs={{0,4},{1,5},{2,6},{3,7},{4,0},{5,1},{6,2},{7,3},{8,12},{9,13},{10,... | collective-permute-start | bytes 159752 | tf_op jit(solution)/shard_map/ppermute | solution.py:24
  30.6 3.7 %collective-permute-done.18.refs_1_ = bf16[208,128]{1,0:T(8,128)(2,1)S(1)} collective-permute-done((bf16[208,128]{1,0:T(8,128)(2,1)S(1)}, bf16[208,128]{1,0:T(8,128)(2,1)S(1)}, u32[]{:S(2)}, u32[]{:S(2)}) %collective-permute-start.18) | collective-permute-done | bytes 53280 | tf_op jit(solution)/shard_map/ppermute | solution.py:24
  34.3 0.0 collective-permute-done.19.refs_2_
  34.3 0.7 %collective-permute-done.20.refs_3_ = bf16[208,128]{1,0:T(8,128)(2,1)S(1)} collective-permute-done((bf16[208,128]{1,0:T(8,128)(2,1)S(1)}, bf16[208,128]{1,0:T(8,128)(2,1)S(1)}, u32[]{:S(2)}, u32[]{:S(2)}) %collective-permute-start.20) | collective-permute-done | bytes 53280 | tf_op jit(solution)/shard_map/ppermute | solution.py:24
  35.0 1.0 %home_merge.1 = bf16[4,6144]{1,0:T(4,128)(2,1)} custom-call(bf16[208,128]{1,0:T(8,128)(2,1)S(1)} %get-tuple-element.9.refs_0_, bf16[208,128]{1,0:T(8,128)(2,1)S(1)} %collective-permute-done.18.refs_1_, bf16[208,128]{1,0:T(8,128)(2,1)S(1)} %collective-permute-done.19.refs_2_, bf16[208,128]{1,0:T(8,128)(2,1)S(1)} %collective-permute-done.20.refs_3_), custom_call_target="tpu_custom_call" | custom-call | tf_op jit(solution)/shard_map/home_merge/pallas_call | solution.py:300
  (8 shorter events, 0.0 us)
Async XLA Ops:
  0.0 17.8 %copy-start.2 = (bf16[4,6144]{1,0:T(4,128)(2,1)S(1)}, bf16[4,6144]{1,0:T(4,128)(2,1)}, u32[]{:S(2)}) copy-start(bf16[4,6144]{1,0:T(4,128)(2,1)} %refs_2_.1) | copy-start | bytes 147460
  0.0 17.8 %copy-start.3 = (s32[8]{0:T(128)S(1)}, s32[8]{0:T(128)}, u32[]{:S(2)}) copy-start(s32[8]{0:T(128)} %param.8) | copy-start | bytes 100
  0.0 17.8 %copy-start.4 = (s32[8]{0:T(128)S(1)}, s32[8]{0:T(128)}, u32[]{:S(2)}) copy-start(s32[8]{0:T(128)} %param.9) | copy-start | bytes 100
  0.0 17.8 %copy-start = (bf16[8,128,1024]{2,1,0:T(8,128)(2,1)S(1)}, bf16[8,128,1024]{2,1,0:T(8,128)(2,1)}, u32[]{:S(2)}) copy-start(bf16[8,128,1024]{2,1,0:T(8,128)(2,1)} %refs_3_.1) | copy-start | bytes 6291460
  0.0 17.8 %copy-start.1 = (bf16[8,128,1024]{2,1,0:T(8,128)(2,1)S(1)}, bf16[8,128,1024]{2,1,0:T(8,128)(2,1)}, u32[]{:S(2)}) copy-start(bf16[8,128,1024]{2,1,0:T(8,128)(2,1)} %refs_4_.1) | copy-start | bytes 6291460
  0.0 7.5 %collective-permute-start.7 = (bf16[4,6144]{1,0:T(4,128)(2,1)}, bf16[4,6144]{1,0:T(4,128)(2,1)S(1)}, u32[]{:S(2)}, u32[]{:S(2)}) collective-permute-start(bf16[4,6144]{1,0:T(4,128)(2,1)} %refs_2_.1), channel_id=1, source_target_pairs={{0,8},{1,9},{2,10},{3,11},{4,12},{5,13},{6,14},{7,15},{8,0},{9,1},... | collective-permute-start | bytes 147464 | tf_op jit(solution)/shard_map/ppermute | solution.py:24
  4.2 4.6 %collective-permute-start.3 = (bf16[4,6144]{1,0:T(4,128)(2,1)}, bf16[4,6144]{1,0:T(4,128)(2,1)S(1)}, u32[]{:S(2)}, u32[]{:S(2)}) collective-permute-start(bf16[4,6144]{1,0:T(4,128)(2,1)} %refs_2_.1), channel_id=1, source_target_pairs={{0,4},{1,5},{2,6},{3,7},{4,0},{5,1},{6,2},{7,3},{8,12},{9,13},{10,... | collective-permute-start | bytes 147464 | tf_op jit(solution)/shard_map/ppermute | solution.py:24
  5.7 6.1 %collective-permute-start.11 = (bf16[4,6144]{1,0:T(4,128)(2,1)}, bf16[4,6144]{1,0:T(4,128)(2,1)S(1)}, u32[]{:S(2)}, u32[]{:S(2)}) collective-permute-start(bf16[4,6144]{1,0:T(4,128)(2,1)} %refs_2_.1), channel_id=1, source_target_pairs={{0,12},{1,13},{2,14},{3,15},{4,8},{5,9},{6,10},{7,11},{8,4},{9,5},... | collective-permute-start | bytes 147464 | tf_op jit(solution)/shard_map/ppermute | solution.py:24
  5.7 6.1 %collective-permute-start.1 = (bf16[4,6144]{1,0:T(4,128)(2,1)}, bf16[4,6144]{1,0:T(4,128)(2,1)S(1)}, u32[]{:S(2)}, u32[]{:S(2)}) collective-permute-start(bf16[4,6144]{1,0:T(4,128)(2,1)} %refs_2_.1), channel_id=1, source_target_pairs={{0,2},{1,3},{2,0},{3,1},{4,6},{5,7},{6,4},{7,5},{8,10},{9,11},{10,... | collective-permute-start | bytes 147464 | tf_op jit(solution)/shard_map/ppermute | solution.py:24
  7.5 4.9 %collective-permute-start = (bf16[4,6144]{1,0:T(4,128)(2,1)}, bf16[4,6144]{1,0:T(4,128)(2,1)S(1)}, u32[]{:S(2)}, u32[]{:S(2)}) collective-permute-start(bf16[4,6144]{1,0:T(4,128)(2,1)} %refs_2_.1), channel_id=1, source_target_pairs={{0,1},{1,0},{2,3},{3,2},{4,5},{5,4},{6,7},{7,6},{8,9},{9,8},{10,11... | collective-permute-start | bytes 147464 | tf_op jit(solution)/shard_map/ppermute | solution.py:24
  7.5 4.9 %collective-permute-start.9 = (bf16[4,6144]{1,0:T(4,128)(2,1)S(1)}, bf16[4,6144]{1,0:T(4,128)(2,1)S(1)}, u32[]{:S(2)}, u32[]{:S(2)}) collective-permute-start(bf16[4,6144]{1,0:T(4,128)(2,1)S(1)} %collective-permute-done.7.refs_7_), channel_id=1, source_target_pairs={{0,2},{1,3},{2,0},{3,1},{4,6},{5,7},{6,4},{7,5},{8,10},{9,11},{10,... | collective-permute-start | bytes 147464 | tf_op jit(solution)/shard_map/ppermute | solution.py:24
  8.8 5.2 %collective-permute-start.5 = (bf16[4,6144]{1,0:T(4,128)(2,1)S(1)}, bf16[4,6144]{1,0:T(4,128)(2,1)S(1)}, u32[]{:S(2)}, u32[]{:S(2)}) collective-permute-start(bf16[4,6144]{1,0:T(4,128)(2,1)S(1)} %collective-permute-done.3.refs_3_), channel_id=1, source_target_pairs={{0,2},{1,3},{2,0},{3,1},{4,6},{5,7},{6,4},{7,5},{8,10},{9,11},{10,... | collective-permute-start | bytes 147464 | tf_op jit(solution)/shard_map/ppermute | solution.py:24
  11.8 2.3 %collective-permute-start.12 = (bf16[4,6144]{1,0:T(4,128)(2,1)S(1)}, bf16[4,6144]{1,0:T(4,128)(2,1)S(1)}, u32[]{:S(2)}, u32[]{:S(2)}) collective-permute-start(bf16[4,6144]{1,0:T(4,128)(2,1)S(1)} %collective-permute-done.11.refs_11_), channel_id=1, source_target_pairs={{0,1},{1,0},{2,3},{3,2},{4,5},{5,4},{6,7},{7,6},{8,9},{9,8},{10,11... | collective-permute-start | bytes 147464 | tf_op jit(solution)/shard_map/ppermute | solution.py:24
  11.8 2.6 %collective-permute-start.4 = (bf16[4,6144]{1,0:T(4,128)(2,1)S(1)}, bf16[4,6144]{1,0:T(4,128)(2,1)S(1)}, u32[]{:S(2)}, u32[]{:S(2)}) collective-permute-start(bf16[4,6144]{1,0:T(4,128)(2,1)S(1)} %collective-permute-done.3.refs_3_), channel_id=1, source_target_pairs={{0,1},{1,0},{2,3},{3,2},{4,5},{5,4},{6,7},{7,6},{8,9},{9,8},{10,11... | collective-permute-start | bytes 147464 | tf_op jit(solution)/shard_map/ppermute | solution.py:24
  12.4 4.2 %collective-permute-start.8 = (bf16[4,6144]{1,0:T(4,128)(2,1)S(1)}, bf16[4,6144]{1,0:T(4,128)(2,1)S(1)}, u32[]{:S(2)}, u32[]{:S(2)}) collective-permute-start(bf16[4,6144]{1,0:T(4,128)(2,1)S(1)} %collective-permute-done.7.refs_7_), channel_id=1, source_target_pairs={{0,1},{1,0},{2,3},{3,2},{4,5},{5,4},{6,7},{7,6},{8,9},{9,8},{10,11... | collective-permute-start | bytes 147464 | tf_op jit(solution)/shard_map/ppermute | solution.py:24
  12.4 4.1 %collective-permute-start.13 = (bf16[4,6144]{1,0:T(4,128)(2,1)S(1)}, bf16[4,6144]{1,0:T(4,128)(2,1)S(1)}, u32[]{:S(2)}, u32[]{:S(2)}) collective-permute-start(bf16[4,6144]{1,0:T(4,128)(2,1)S(1)} %collective-permute-done.11.refs_11_), channel_id=1, source_target_pairs={{0,2},{1,3},{2,0},{3,1},{4,6},{5,7},{6,4},{7,5},{8,10},{9,11},{10,... | collective-permute-start | bytes 147464 | tf_op jit(solution)/shard_map/ppermute | solution.py:24
  14.0 2.6 %collective-permute-start.2 = (bf16[4,6144]{1,0:T(4,128)(2,1)S(1)}, bf16[4,6144]{1,0:T(4,128)(2,1)S(1)}, u32[]{:S(2)}, u32[]{:S(2)}) collective-permute-start(bf16[4,6144]{1,0:T(4,128)(2,1)S(1)} %collective-permute-done.1.refs_1_), channel_id=1, source_target_pairs={{0,1},{1,0},{2,3},{3,2},{4,5},{5,4},{6,7},{7,6},{8,9},{9,8},{10,11... | collective-permute-start | bytes 147464 | tf_op jit(solution)/shard_map/ppermute | solution.py:24
  14.1 2.4 %collective-permute-start.10 = (bf16[4,6144]{1,0:T(4,128)(2,1)S(1)}, bf16[4,6144]{1,0:T(4,128)(2,1)S(1)}, u32[]{:S(2)}, u32[]{:S(2)}) collective-permute-start(bf16[4,6144]{1,0:T(4,128)(2,1)S(1)} %collective-permute-done.9.refs_9_), channel_id=1, source_target_pairs={{0,1},{1,0},{2,3},{3,2},{4,5},{5,4},{6,7},{7,6},{8,9},{9,8},{10,11... | collective-permute-start | bytes 147464 | tf_op jit(solution)/shard_map/ppermute | solution.py:24
  14.5 2.1 %collective-permute-start.6 = (bf16[4,6144]{1,0:T(4,128)(2,1)S(1)}, bf16[4,6144]{1,0:T(4,128)(2,1)S(1)}, u32[]{:S(2)}, u32[]{:S(2)}) collective-permute-start(bf16[4,6144]{1,0:T(4,128)(2,1)S(1)} %collective-permute-done.5.refs_5_), channel_id=1, source_target_pairs={{0,1},{1,0},{2,3},{3,2},{4,5},{5,4},{6,7},{7,6},{8,9},{9,8},{10,11... | collective-permute-start | bytes 147464 | tf_op jit(solution)/shard_map/ppermute | solution.py:24
  16.5 1.2 %collective-permute-start.14 = (bf16[4,6144]{1,0:T(4,128)(2,1)S(1)}, bf16[4,6144]{1,0:T(4,128)(2,1)S(1)}, u32[]{:S(2)}, u32[]{:S(2)}) collective-permute-start(bf16[4,6144]{1,0:T(4,128)(2,1)S(1)} %collective-permute-done.13.refs_0_), channel_id=1, source_target_pairs={{0,1},{1,0},{2,3},{3,2},{4,5},{5,4},{6,7},{7,6},{8,9},{9,8},{10,11... | collective-permute-start | bytes 147464 | tf_op jit(solution)/shard_map/ppermute | solution.py:24
  19.0 5.2 %collective-permute-start.16 = (bf16[432,128]{1,0:T(8,128)(2,1)S(1)}, bf16[432,128]{1,0:T(8,128)(2,1)S(1)}, u32[]{:S(2)}, u32[]{:S(2)}) collective-permute-start(bf16[432,128]{1,0:T(8,128)(2,1)S(1)} %attend.1.refs_0_), channel_id=1, source_target_pairs={{0,2},{1,3},{2,0},{3,1},{4,6},{5,7},{6,4},{7,5},{8,10},{9,11},{10,... | collective-permute-start | bytes 331784 | tf_op jit(solution)/shard_map/ppermute | solution.py:24
  20.6 3.6 %collective-permute-start.15 = (bf16[432,128]{1,0:T(8,128)(2,1)S(1)}, bf16[432,128]{1,0:T(8,128)(2,1)S(1)}, u32[]{:S(2)}, u32[]{:S(2)}) collective-permute-start(bf16[432,128]{1,0:T(8,128)(2,1)S(1)} %attend.1.refs_0_), channel_id=1, source_target_pairs={{0,1},{1,0},{2,3},{3,2},{4,5},{5,4},{6,7},{7,6},{8,9},{9,8},{10,11... | collective-permute-start | bytes 331784 | tf_op jit(solution)/shard_map/ppermute | solution.py:24
  24.2 1.3 %collective-permute-start.17 = (bf16[432,128]{1,0:T(8,128)(2,1)S(1)}, bf16[432,128]{1,0:T(8,128)(2,1)S(1)}, u32[]{:S(2)}, u32[]{:S(2)}) collective-permute-start(bf16[432,128]{1,0:T(8,128)(2,1)S(1)} %collective-permute-done.16.refs_2_), channel_id=1, source_target_pairs={{0,1},{1,0},{2,3},{3,2},{4,5},{5,4},{6,7},{7,6},{8,9},{9,8},{10,11... | collective-permute-start | bytes 331784 | tf_op jit(solution)/shard_map/ppermute | solution.py:24
  26.6 7.8 %collective-permute-start.18 = (bf16[208,128]{1,0:T(8,128)(2,1)S(1)}, bf16[208,128]{1,0:T(8,128)(2,1)S(1)}, u32[]{:S(2)}, u32[]{:S(2)}) collective-permute-start(bf16[208,128]{1,0:T(8,128)(2,1)S(1)} %get-tuple-element.10), channel_id=1, source_target_pairs={{0,8},{1,9},{2,10},{3,11},{4,12},{5,13},{6,14},{7,15},{8,0},{9,1},... | collective-permute-start | bytes 159752 | tf_op jit(solution)/shard_map/ppermute | solution.py:24
  28.0 6.3 %collective-permute-start.19 = (bf16[208,128]{1,0:T(8,128)(2,1)S(1)}, bf16[208,128]{1,0:T(8,128)(2,1)S(1)}, u32[]{:S(2)}, u32[]{:S(2)}) collective-permute-start(bf16[208,128]{1,0:T(8,128)(2,1)S(1)} %get-tuple-element.11), channel_id=1, source_target_pairs={{0,12},{1,13},{2,14},{3,15},{4,8},{5,9},{6,10},{7,11},{8,4},{9,5},... | collective-permute-start | bytes 159752 | tf_op jit(solution)/shard_map/ppermute | solution.py:24
  30.1 4.9 %collective-permute-start.20 = (bf16[208,128]{1,0:T(8,128)(2,1)S(1)}, bf16[208,128]{1,0:T(8,128)(2,1)S(1)}, u32[]{:S(2)}, u32[]{:S(2)}) collective-permute-start(bf16[208,128]{1,0:T(8,128)(2,1)S(1)} %get-tuple-element.12), channel_id=1, source_target_pairs={{0,4},{1,5},{2,6},{3,7},{4,0},{5,1},{6,2},{7,3},{8,12},{9,13},{10,... | collective-permute-start | bytes 159752 | tf_op jit(solution)/shard_map/ppermute | solution.py:24
where the time goes:
time: 36.2 us; the launch traced here: 36 us
  starting transfers between devices  18.4 us (51%)
  waiting for transfers between devices  14.1 us (39%)
  Pallas kernels  3.5 us (10%)
    ppermute x21, starting transfers between devices, exchange(): return lax.ppermute(x, 'seq', [(i, i ^ step) for i in range(count)])  18.4 us
    ppermute x21, waiting for transfers between devices, exchange(): return lax.ppermute(x, 'seq', [(i, i ^ step) for i in range(count)])  14.1 us
    pallas_call x1, Pallas kernels, attend(): pl.pallas_call(functools.partial(attend_kernel, len(late), by_xor), name=...  1.21 us
    pallas_call x1, Pallas kernels, layer_merge(): pl.pallas_call(functools.partial(layer_kernel, req_dev), name='layer_merg...  1.06 us
    pallas_call x1, Pallas kernels, home_merge(): pl.pallas_call(home_kernel, name='home_merge', out_shape=jax.ShapeDtypeSt...  0.99 us
  transfers between devices with their start and end apart: 21, of which 7 were waited for; matrix products, arithmetic and copies ran while one was open for 0% of the time, Pallas kernels for 1%

commit v1 on v0

--- a/solution.py
+++ b/solution.py
@@ -139,7 +139,9 @@
     index = jnp.concatenate(index + [jnp.zeros((1, LANES - 2 * pages), jnp.int32)], axis=1)
     index = pltpu.roll(index.astype(jnp.float32), 6 * pages, 1)
     inside = jnp.logical_and(lane >= 6 * pages, lane < 8 * pages)
-    send[HEADS * pages :, :] = jnp.where(inside, index, stats).astype(send.dtype)
+    stats = jnp.where(inside, index, stats)
+    stats = stats[: HEADS // 2] + pltpu.roll(stats[HEADS // 2 :], HALF, 1)
+    send[HEADS * pages :, :] = stats.astype(send.dtype)
 
     for p in range(pages):
         mixed = lax.dot_general(
@@ -158,7 +160,7 @@
     return pl.pallas_call(
         functools.partial(attend_kernel, len(late), by_xor),
         name="attend",
-        out_shape=jax.ShapeDtypeStruct(((pages + 1) * HEADS, LANES), jnp.bfloat16),
+        out_shape=jax.ShapeDtypeStruct((pages * HEADS + HEADS // 2, LANES), jnp.bfloat16),
         in_specs=[vmem] * (len(late) + 5),
         out_specs=vmem,
         scratch_shapes=[
@@ -171,7 +173,7 @@
 
 
 def page_tables(blocks, slots, req_dev):
-    pages = blocks[0].shape[0] // HEADS - 1
+    pages = blocks[0].shape[0] // HEADS
     me = lax.axis_index("seq")
     lane = lax.broadcasted_iota(jnp.int32, (HEADS, LANES), 1)
     peaks = jnp.full((HEADS, LANES), FLOOR, jnp.float32)
@@ -180,6 +182,7 @@
     local = jnp.zeros((1, LANES), jnp.float32)
     for s, block in enumerate(blocks):
         stats = block[HEADS * pages :, :].astype(jnp.float32)
+        stats = jnp.concatenate([stats, pltpu.roll(stats, HALF, 1)], axis=0)
         whole = stats + pltpu.roll(stats, LANES - 2 * pages, 1) + pltpu.roll(stats, LANES - 4 * pages, 1)
         inside = jnp.logical_and(lane >= pages * s, lane < pages * (s + 1))
         peaks = jnp.where(inside, pltpu.roll(whole, (pages * s) % LANES, 1), peaks)
@@ -194,7 +197,7 @@
 
 def layer_kernel(req_dev, *refs):
     blocks, outs, (sums, place, index, sem) = refs[:LAYER], refs[LAYER:-4], refs[-4:]
-    pages = blocks[0].shape[0] // HEADS - 1
+    pages = blocks[0].shape[0] // HEADS
     slots = sums.shape[0] - 1
     lane = lax.broadcasted_iota(jnp.int32, (HEADS, LANES), 1)
     peaks, totals, where = page_tables(blocks, slots, req_dev)

time: 36.2 us -> 36 us (level)
  no operation moved by 1% of the time
where the time goes in v1:
time: 36 us; the launch traced here: 35.9 us
  starting transfers between devices  18.3 us (51%)
  waiting for transfers between devices  13.9 us (39%)
  Pallas kernels  3.52 us (10%)
    ppermute x21, starting transfers between devices, exchange(): return lax.ppermute(x, 'seq', [(i, i ^ step) for i in range(count)])  18.3 us
    ppermute x21, waiting for transfers between devices, exchange(): return lax.ppermute(x, 'seq', [(i, i ^ step) for i in range(count)])  13.9 us
    pallas_call x1, Pallas kernels, attend(): pl.pallas_call(functools.partial(attend_kernel, len(late), by_xor), name=...  1.24 us
    pallas_call x1, Pallas kernels, layer_merge(): pl.pallas_call(functools.partial(layer_kernel, req_dev), name='layer_merg...  1.05 us
    pallas_call x1, Pallas kernels, home_merge(): pl.pallas_call(home_kernel, name='home_merge', out_shape=jax.ShapeDtypeSt...  0.99 us
  transfers between devices with their start and end apart: 21, of which 7 were waited for; matrix products, arithmetic and copies ran while one was open for 0% of the time, Pallas kernels for 1%

profile of v1, /device:TPU:0, one launch (start us, length us, event | category | flops | bytes accessed | tf_op | source)
XLA Modules:
  0.0 35.9 jit_solution(6758907513194340370)
XLA Ops:
  0.0 4.1 %collective-permute-start.7 = (bf16[4,6144]{1,0:T(4,128)(2,1)}, bf16[4,6144]{1,0:T(4,128)(2,1)S(1)}, u32[]{:S(2)}, u32[]{:S(2)}) collective-permute-start(bf16[4,6144]{1,0:T(4,128)(2,1)} %refs_2_.1), channel_id=1, source_target_pairs={{0,8},{1,9},{2,10},{3,11},{4,12},{5,13},{6,14},{7,15},{8,0},{9,1},... | collective-permute-start | bytes 147464 | tf_op jit(solution)/shard_map/ppermute | solution.py:24
  4.2 1.6 %collective-permute-start.3 = (bf16[4,6144]{1,0:T(4,128)(2,1)}, bf16[4,6144]{1,0:T(4,128)(2,1)S(1)}, u32[]{:S(2)}, u32[]{:S(2)}) collective-permute-start(bf16[4,6144]{1,0:T(4,128)(2,1)} %refs_2_.1), channel_id=1, source_target_pairs={{0,4},{1,5},{2,6},{3,7},{4,0},{5,1},{6,2},{7,3},{8,12},{9,13},{10,... | collective-permute-start | bytes 147464 | tf_op jit(solution)/shard_map/ppermute | solution.py:24
  5.7 0.0 collective-permute-start.11
  5.7 1.7 %collective-permute-start.1 = (bf16[4,6144]{1,0:T(4,128)(2,1)}, bf16[4,6144]{1,0:T(4,128)(2,1)S(1)}, u32[]{:S(2)}, u32[]{:S(2)}) collective-permute-start(bf16[4,6144]{1,0:T(4,128)(2,1)} %refs_2_.1), channel_id=1, source_target_pairs={{0,2},{1,3},{2,0},{3,1},{4,6},{5,7},{6,4},{7,5},{8,10},{9,11},{10,... | collective-permute-start | bytes 147464 | tf_op jit(solution)/shard_map/ppermute | solution.py:24
  7.5 0.0 collective-permute-start
  7.5 0.0 collective-permute-done.7.refs_7_
  7.5 1.3 %collective-permute-start.9 = (bf16[4,6144]{1,0:T(4,128)(2,1)S(1)}, bf16[4,6144]{1,0:T(4,128)(2,1)S(1)}, u32[]{:S(2)}, u32[]{:S(2)}) collective-permute-start(bf16[4,6144]{1,0:T(4,128)(2,1)S(1)} %collective-permute-done.7.refs_7_), channel_id=1, source_target_pairs={{0,2},{1,3},{2,0},{3,1},{4,6},{5,7},{6,4},{7,5},{8,10},{9,11},{10,... | collective-permute-start | bytes 147464 | tf_op jit(solution)/shard_map/ppermute | solution.py:24
  8.8 0.0 collective-permute-done.3.refs_3_
  8.8 1.2 %collective-permute-start.5 = (bf16[4,6144]{1,0:T(4,128)(2,1)S(1)}, bf16[4,6144]{1,0:T(4,128)(2,1)S(1)}, u32[]{:S(2)}, u32[]{:S(2)}) collective-permute-start(bf16[4,6144]{1,0:T(4,128)(2,1)S(1)} %collective-permute-done.3.refs_3_), channel_id=1, source_target_pairs={{0,2},{1,3},{2,0},{3,1},{4,6},{5,7},{6,4},{7,5},{8,10},{9,11},{10,... | collective-permute-start | bytes 147464 | tf_op jit(solution)/shard_map/ppermute | solution.py:24
  10.0 1.9 %collective-permute-done.11.refs_11_ = bf16[4,6144]{1,0:T(4,128)(2,1)S(1)} collective-permute-done((bf16[4,6144]{1,0:T(4,128)(2,1)}, bf16[4,6144]{1,0:T(4,128)(2,1)S(1)}, u32[]{:S(2)}, u32[]{:S(2)}) %collective-permute-start.11) | collective-permute-done | bytes 49184 | tf_op jit(solution)/shard_map/ppermute | solution.py:24
  11.8 0.0 collective-permute-start.12
  11.8 0.0 collective-permute-done.1.refs_1_
  11.8 0.5 %collective-permute-start.4 = (bf16[4,6144]{1,0:T(4,128)(2,1)S(1)}, bf16[4,6144]{1,0:T(4,128)(2,1)S(1)}, u32[]{:S(2)}, u32[]{:S(2)}) collective-permute-start(bf16[4,6144]{1,0:T(4,128)(2,1)S(1)} %collective-permute-done.3.refs_3_), channel_id=1, source_target_pairs={{0,1},{1,0},{2,3},{3,2},{4,5},{5,4},{6,7},{7,6},{8,9},{9,8},{10,11... | collective-permute-start | bytes 147464 | tf_op jit(solution)/shard_map/ppermute | solution.py:24
  12.4 0.0 collective-permute-done.refs_0_
  12.4 0.1 collective-permute-start.8
  12.4 0.0 collective-permute-done.9.refs_9_
  12.4 1.5 %collective-permute-start.13 = (bf16[4,6144]{1,0:T(4,128)(2,1)S(1)}, bf16[4,6144]{1,0:T(4,128)(2,1)S(1)}, u32[]{:S(2)}, u32[]{:S(2)}) collective-permute-start(bf16[4,6144]{1,0:T(4,128)(2,1)S(1)} %collective-permute-done.11.refs_11_), channel_id=1, source_target_pairs={{0,2},{1,3},{2,0},{3,1},{4,6},{5,7},{6,4},{7,5},{8,10},{9,11},{10,... | collective-permute-start | bytes 147464 | tf_op jit(solution)/shard_map/ppermute | solution.py:24
  13.9 0.0 collective-permute-done.5.refs_5_
  14.0 0.2 collective-permute-start.2
  14.1 0.0 collective-permute-done.12.refs_12_
  14.1 0.3 collective-permute-start.10
  14.5 0.0 collective-permute-done.4.refs_4_
  14.5 0.2 collective-permute-start.6
  14.6 1.9 %collective-permute-done.13.refs_0_ = bf16[4,6144]{1,0:T(4,128)(2,1)S(1)} collective-permute-done((bf16[4,6144]{1,0:T(4,128)(2,1)S(1)}, bf16[4,6144]{1,0:T(4,128)(2,1)S(1)}, u32[]{:S(2)}, u32[]{:S(2)}) %collective-permute-start.13) | collective-permute-done | bytes 49184 | tf_op jit(solution)/shard_map/ppermute | solution.py:24
  16.5 0.0 collective-permute-start.14
  16.5 0.0 collective-permute-done.8.refs_8_
  16.5 0.0 collective-permute-done.2.refs_2_
  16.5 0.0 collective-permute-done.10.refs_10_
  16.5 0.0 collective-permute-done.6.refs_6_
  16.6 0.3 stage.1.held
  16.8 0.9 %collective-permute-done.14.refs_1_ = bf16[4,6144]{1,0:T(4,128)(2,1)S(1)} collective-permute-done((bf16[4,6144]{1,0:T(4,128)(2,1)S(1)}, bf16[4,6144]{1,0:T(4,128)(2,1)S(1)}, u32[]{:S(2)}, u32[]{:S(2)}) %collective-permute-start.14) | collective-permute-done | bytes 49184 | tf_op jit(solution)/shard_map/ppermute | solution.py:24
  17.8 0.0 copy-done.4
  17.8 0.0 copy-done
  17.8 1.2 %attend.1.refs_0_ = bf16[408,128]{1,0:T(8,128)(2,1)S(1)} custom-call(s32[1,8]{1,0:T(1,128)S(1)} %bitcast.2, s32[1,8]{1,0:T(1,128)S(1)} %bitcast.3, bf16[13,4,48,128]{3,2,1,0:T(8,128)(2,1)S(1)} %stage.1.held, bf16[4,6144]{1,0:T(4,128)(2,1)S(1)} %collective-permute-done.13.refs_0_, bf16[4,6144]{1,0:T(4,128)(2,1)S(1)} %collective-permute-done.14.refs_1_, ...), custom_call_target="tpu_custom_call" | custom-call | tf_op jit(solution)/shard_map/attend/pallas_call | solution.py:160
  19.0 1.6 %collective-permute-start.16 = (bf16[408,128]{1,0:T(8,128)(2,1)S(1)}, bf16[408,128]{1,0:T(8,128)(2,1)S(1)}, u32[]{:S(2)}, u32[]{:S(2)}) collective-permute-start(bf16[408,128]{1,0:T(8,128)(2,1)S(1)} %attend.1.refs_0_), channel_id=1, source_target_pairs={{0,2},{1,3},{2,0},{3,1},{4,6},{5,7},{6,4},{7,5},{8,10},{9,11},{10,... | collective-permute-start | bytes 313352 | tf_op jit(solution)/shard_map/ppermute | solution.py:24
  20.6 0.0 collective-permute-start.15
  20.6 3.5 %collective-permute-done.16.refs_2_ = bf16[408,128]{1,0:T(8,128)(2,1)S(1)} collective-permute-done((bf16[408,128]{1,0:T(8,128)(2,1)S(1)}, bf16[408,128]{1,0:T(8,128)(2,1)S(1)}, u32[]{:S(2)}, u32[]{:S(2)}) %collective-permute-start.16) | collective-permute-done | bytes 104480 | tf_op jit(solution)/shard_map/ppermute | solution.py:24
  24.0 0.0 collective-permute-start.17
  24.0 0.0 collective-permute-done.15.refs_1_
  24.0 1.3 %collective-permute-done.17.refs_3_ = bf16[408,128]{1,0:T(8,128)(2,1)S(1)} collective-permute-done((bf16[408,128]{1,0:T(8,128)(2,1)S(1)}, bf16[408,128]{1,0:T(8,128)(2,1)S(1)}, u32[]{:S(2)}, u32[]{:S(2)}) %collective-permute-start.17) | collective-permute-done | bytes 104480 | tf_op jit(solution)/shard_map/ppermute | solution.py:24
  25.4 1.0 %layer_merge.1 = (bf16[208,128]{1,0:T(8,128)(2,1)S(1)}, bf16[208,128]{1,0:T(8,128)(2,1)S(1)}, bf16[208,128]{1,0:T(8,128)(2,1)S(1)}, bf16[208,128]{1,0:T(8,128)(2,1)S(1)}) custom-call(bf16[408,128]{1,0:T(8,128)(2,1)S(1)} %attend.1.refs_0_, bf16[408,128]{1,0:T(8,128)(2,1)S(1)} %collective-permute-done.15.refs_1_, ...), custom_call_target="tpu_custom_call" | custom-call | tf_op jit(solution)/shard_map/layer_merge/pallas_call | solution.py:253
  26.4 1.5 %collective-permute-start.18 = (bf16[208,128]{1,0:T(8,128)(2,1)S(1)}, bf16[208,128]{1,0:T(8,128)(2,1)S(1)}, u32[]{:S(2)}, u32[]{:S(2)}) collective-permute-start(bf16[208,128]{1,0:T(8,128)(2,1)S(1)} %get-tuple-element.10), channel_id=1, source_target_pairs={{0,8},{1,9},{2,10},{3,11},{4,12},{5,13},{6,14},{7,15},{8,0},{9,1},... | collective-permute-start | bytes 159752 | tf_op jit(solution)/shard_map/ppermute | solution.py:24
  27.9 2.1 %collective-permute-start.19 = (bf16[208,128]{1,0:T(8,128)(2,1)S(1)}, bf16[208,128]{1,0:T(8,128)(2,1)S(1)}, u32[]{:S(2)}, u32[]{:S(2)}) collective-permute-start(bf16[208,128]{1,0:T(8,128)(2,1)S(1)} %get-tuple-element.11), channel_id=1, source_target_pairs={{0,12},{1,13},{2,14},{3,15},{4,8},{5,9},{6,10},{7,11},{8,4},{9,5},... | collective-permute-start | bytes 159752 | tf_op jit(solution)/shard_map/ppermute | solution.py:24
  30.0 0.5 %collective-permute-start.20 = (bf16[208,128]{1,0:T(8,128)(2,1)S(1)}, bf16[208,128]{1,0:T(8,128)(2,1)S(1)}, u32[]{:S(2)}, u32[]{:S(2)}) collective-permute-start(bf16[208,128]{1,0:T(8,128)(2,1)S(1)} %get-tuple-element.12), channel_id=1, source_target_pairs={{0,4},{1,5},{2,6},{3,7},{4,0},{5,1},{6,2},{7,3},{8,12},{9,13},{10,... | collective-permute-start | bytes 159752 | tf_op jit(solution)/shard_map/ppermute | solution.py:24
  30.4 3.7 %collective-permute-done.18.refs_1_ = bf16[208,128]{1,0:T(8,128)(2,1)S(1)} collective-permute-done((bf16[208,128]{1,0:T(8,128)(2,1)S(1)}, bf16[208,128]{1,0:T(8,128)(2,1)S(1)}, u32[]{:S(2)}, u32[]{:S(2)}) %collective-permute-start.18) | collective-permute-done | bytes 53280 | tf_op jit(solution)/shard_map/ppermute | solution.py:24
  34.2 0.0 collective-permute-done.19.refs_2_
  34.2 0.7 %collective-permute-done.20.refs_3_ = bf16[208,128]{1,0:T(8,128)(2,1)S(1)} collective-permute-done((bf16[208,128]{1,0:T(8,128)(2,1)S(1)}, bf16[208,128]{1,0:T(8,128)(2,1)S(1)}, u32[]{:S(2)}, u32[]{:S(2)}) %collective-permute-start.20) | collective-permute-done | bytes 53280 | tf_op jit(solution)/shard_map/ppermute | solution.py:24
  34.9 1.0 %home_merge.1 = bf16[4,6144]{1,0:T(4,128)(2,1)} custom-call(bf16[208,128]{1,0:T(8,128)(2,1)S(1)} %get-tuple-element.9.refs_0_, bf16[208,128]{1,0:T(8,128)(2,1)S(1)} %collective-permute-done.18.refs_1_, bf16[208,128]{1,0:T(8,128)(2,1)S(1)} %collective-permute-done.19.refs_2_, bf16[208,128]{1,0:T(8,128)(2,1)S(1)} %collective-permute-done.20.refs_3_), custom_call_target="tpu_custom_call" | custom-call | tf_op jit(solution)/shard_map/home_merge/pallas_call | solution.py:303
  (8 shorter events, 0.0 us)
Async XLA Ops:
  0.0 17.8 %copy-start.2 = (bf16[4,6144]{1,0:T(4,128)(2,1)S(1)}, bf16[4,6144]{1,0:T(4,128)(2,1)}, u32[]{:S(2)}) copy-start(bf16[4,6144]{1,0:T(4,128)(2,1)} %refs_2_.1) | copy-start | bytes 147460
  0.0 17.8 %copy-start.3 = (s32[8]{0:T(128)S(1)}, s32[8]{0:T(128)}, u32[]{:S(2)}) copy-start(s32[8]{0:T(128)} %param.8) | copy-start | bytes 100
  0.0 17.8 %copy-start.4 = (s32[8]{0:T(128)S(1)}, s32[8]{0:T(128)}, u32[]{:S(2)}) copy-start(s32[8]{0:T(128)} %param.9) | copy-start | bytes 100
  0.0 17.8 %copy-start = (bf16[8,128,1024]{2,1,0:T(8,128)(2,1)S(1)}, bf16[8,128,1024]{2,1,0:T(8,128)(2,1)}, u32[]{:S(2)}) copy-start(bf16[8,128,1024]{2,1,0:T(8,128)(2,1)} %refs_3_.1) | copy-start | bytes 6291460
  0.0 17.8 %copy-start.1 = (bf16[8,128,1024]{2,1,0:T(8,128)(2,1)S(1)}, bf16[8,128,1024]{2,1,0:T(8,128)(2,1)}, u32[]{:S(2)}) copy-start(bf16[8,128,1024]{2,1,0:T(8,128)(2,1)} %refs_4_.1) | copy-start | bytes 6291460
  0.0 7.5 %collective-permute-start.7 = (bf16[4,6144]{1,0:T(4,128)(2,1)}, bf16[4,6144]{1,0:T(4,128)(2,1)S(1)}, u32[]{:S(2)}, u32[]{:S(2)}) collective-permute-start(bf16[4,6144]{1,0:T(4,128)(2,1)} %refs_2_.1), channel_id=1, source_target_pairs={{0,8},{1,9},{2,10},{3,11},{4,12},{5,13},{6,14},{7,15},{8,0},{9,1},... | collective-permute-start | bytes 147464 | tf_op jit(solution)/shard_map/ppermute | solution.py:24
  4.2 4.6 %collective-permute-start.3 = (bf16[4,6144]{1,0:T(4,128)(2,1)}, bf16[4,6144]{1,0:T(4,128)(2,1)S(1)}, u32[]{:S(2)}, u32[]{:S(2)}) collective-permute-start(bf16[4,6144]{1,0:T(4,128)(2,1)} %refs_2_.1), channel_id=1, source_target_pairs={{0,4},{1,5},{2,6},{3,7},{4,0},{5,1},{6,2},{7,3},{8,12},{9,13},{10,... | collective-permute-start | bytes 147464 | tf_op jit(solution)/shard_map/ppermute | solution.py:24
  5.7 6.1 %collective-permute-start.11 = (bf16[4,6144]{1,0:T(4,128)(2,1)}, bf16[4,6144]{1,0:T(4,128)(2,1)S(1)}, u32[]{:S(2)}, u32[]{:S(2)}) collective-permute-start(bf16[4,6144]{1,0:T(4,128)(2,1)} %refs_2_.1), channel_id=1, source_target_pairs={{0,12},{1,13},{2,14},{3,15},{4,8},{5,9},{6,10},{7,11},{8,4},{9,5},... | collective-permute-start | bytes 147464 | tf_op jit(solution)/shard_map/ppermute | solution.py:24
  5.7 6.1 %collective-permute-start.1 = (bf16[4,6144]{1,0:T(4,128)(2,1)}, bf16[4,6144]{1,0:T(4,128)(2,1)S(1)}, u32[]{:S(2)}, u32[]{:S(2)}) collective-permute-start(bf16[4,6144]{1,0:T(4,128)(2,1)} %refs_2_.1), channel_id=1, source_target_pairs={{0,2},{1,3},{2,0},{3,1},{4,6},{5,7},{6,4},{7,5},{8,10},{9,11},{10,... | collective-permute-start | bytes 147464 | tf_op jit(solution)/shard_map/ppermute | solution.py:24
  7.5 4.9 %collective-permute-start = (bf16[4,6144]{1,0:T(4,128)(2,1)}, bf16[4,6144]{1,0:T(4,128)(2,1)S(1)}, u32[]{:S(2)}, u32[]{:S(2)}) collective-permute-start(bf16[4,6144]{1,0:T(4,128)(2,1)} %refs_2_.1), channel_id=1, source_target_pairs={{0,1},{1,0},{2,3},{3,2},{4,5},{5,4},{6,7},{7,6},{8,9},{9,8},{10,11... | collective-permute-start | bytes 147464 | tf_op jit(solution)/shard_map/ppermute | solution.py:24
  7.5 4.9 %collective-permute-start.9 = (bf16[4,6144]{1,0:T(4,128)(2,1)S(1)}, bf16[4,6144]{1,0:T(4,128)(2,1)S(1)}, u32[]{:S(2)}, u32[]{:S(2)}) collective-permute-start(bf16[4,6144]{1,0:T(4,128)(2,1)S(1)} %collective-permute-done.7.refs_7_), channel_id=1, source_target_pairs={{0,2},{1,3},{2,0},{3,1},{4,6},{5,7},{6,4},{7,5},{8,10},{9,11},{10,... | collective-permute-start | bytes 147464 | tf_op jit(solution)/shard_map/ppermute | solution.py:24
  8.8 5.2 %collective-permute-start.5 = (bf16[4,6144]{1,0:T(4,128)(2,1)S(1)}, bf16[4,6144]{1,0:T(4,128)(2,1)S(1)}, u32[]{:S(2)}, u32[]{:S(2)}) collective-permute-start(bf16[4,6144]{1,0:T(4,128)(2,1)S(1)} %collective-permute-done.3.refs_3_), channel_id=1, source_target_pairs={{0,2},{1,3},{2,0},{3,1},{4,6},{5,7},{6,4},{7,5},{8,10},{9,11},{10,... | collective-permute-start | bytes 147464 | tf_op jit(solution)/shard_map/ppermute | solution.py:24
  11.8 2.3 %collective-permute-start.12 = (bf16[4,6144]{1,0:T(4,128)(2,1)S(1)}, bf16[4,6144]{1,0:T(4,128)(2,1)S(1)}, u32[]{:S(2)}, u32[]{:S(2)}) collective-permute-start(bf16[4,6144]{1,0:T(4,128)(2,1)S(1)} %collective-permute-done.11.refs_11_), channel_id=1, source_target_pairs={{0,1},{1,0},{2,3},{3,2},{4,5},{5,4},{6,7},{7,6},{8,9},{9,8},{10,11... | collective-permute-start | bytes 147464 | tf_op jit(solution)/shard_map/ppermute | solution.py:24
  11.8 2.6 %collective-permute-start.4 = (bf16[4,6144]{1,0:T(4,128)(2,1)S(1)}, bf16[4,6144]{1,0:T(4,128)(2,1)S(1)}, u32[]{:S(2)}, u32[]{:S(2)}) collective-permute-start(bf16[4,6144]{1,0:T(4,128)(2,1)S(1)} %collective-permute-done.3.refs_3_), channel_id=1, source_target_pairs={{0,1},{1,0},{2,3},{3,2},{4,5},{5,4},{6,7},{7,6},{8,9},{9,8},{10,11... | collective-permute-start | bytes 147464 | tf_op jit(solution)/shard_map/ppermute | solution.py:24
  12.4 4.2 %collective-permute-start.8 = (bf16[4,6144]{1,0:T(4,128)(2,1)S(1)}, bf16[4,6144]{1,0:T(4,128)(2,1)S(1)}, u32[]{:S(2)}, u32[]{:S(2)}) collective-permute-start(bf16[4,6144]{1,0:T(4,128)(2,1)S(1)} %collective-permute-done.7.refs_7_), channel_id=1, source_target_pairs={{0,1},{1,0},{2,3},{3,2},{4,5},{5,4},{6,7},{7,6},{8,9},{9,8},{10,11... | collective-permute-start | bytes 147464 | tf_op jit(solution)/shard_map/ppermute | solution.py:24
  12.4 4.1 %collective-permute-start.13 = (bf16[4,6144]{1,0:T(4,128)(2,1)S(1)}, bf16[4,6144]{1,0:T(4,128)(2,1)S(1)}, u32[]{:S(2)}, u32[]{:S(2)}) collective-permute-start(bf16[4,6144]{1,0:T(4,128)(2,1)S(1)} %collective-permute-done.11.refs_11_), channel_id=1, source_target_pairs={{0,2},{1,3},{2,0},{3,1},{4,6},{5,7},{6,4},{7,5},{8,10},{9,11},{10,... | collective-permute-start | bytes 147464 | tf_op jit(solution)/shard_map/ppermute | solution.py:24
  14.0 2.6 %collective-permute-start.2 = (bf16[4,6144]{1,0:T(4,128)(2,1)S(1)}, bf16[4,6144]{1,0:T(4,128)(2,1)S(1)}, u32[]{:S(2)}, u32[]{:S(2)}) collective-permute-start(bf16[4,6144]{1,0:T(4,128)(2,1)S(1)} %collective-permute-done.1.refs_1_), channel_id=1, source_target_pairs={{0,1},{1,0},{2,3},{3,2},{4,5},{5,4},{6,7},{7,6},{8,9},{9,8},{10,11... | collective-permute-start | bytes 147464 | tf_op jit(solution)/shard_map/ppermute | solution.py:24
  14.1 2.4 %collective-permute-start.10 = (bf16[4,6144]{1,0:T(4,128)(2,1)S(1)}, bf16[4,6144]{1,0:T(4,128)(2,1)S(1)}, u32[]{:S(2)}, u32[]{:S(2)}) collective-permute-start(bf16[4,6144]{1,0:T(4,128)(2,1)S(1)} %collective-permute-done.9.refs_9_), channel_id=1, source_target_pairs={{0,1},{1,0},{2,3},{3,2},{4,5},{5,4},{6,7},{7,6},{8,9},{9,8},{10,11... | collective-permute-start | bytes 147464 | tf_op jit(solution)/shard_map/ppermute | solution.py:24
  14.5 2.1 %collective-permute-start.6 = (bf16[4,6144]{1,0:T(4,128)(2,1)S(1)}, bf16[4,6144]{1,0:T(4,128)(2,1)S(1)}, u32[]{:S(2)}, u32[]{:S(2)}) collective-permute-start(bf16[4,6144]{1,0:T(4,128)(2,1)S(1)} %collective-permute-done.5.refs_5_), channel_id=1, source_target_pairs={{0,1},{1,0},{2,3},{3,2},{4,5},{5,4},{6,7},{7,6},{8,9},{9,8},{10,11... | collective-permute-start | bytes 147464 | tf_op jit(solution)/shard_map/ppermute | solution.py:24
  16.5 1.2 %collective-permute-start.14 = (bf16[4,6144]{1,0:T(4,128)(2,1)S(1)}, bf16[4,6144]{1,0:T(4,128)(2,1)S(1)}, u32[]{:S(2)}, u32[]{:S(2)}) collective-permute-start(bf16[4,6144]{1,0:T(4,128)(2,1)S(1)} %collective-permute-done.13.refs_0_), channel_id=1, source_target_pairs={{0,1},{1,0},{2,3},{3,2},{4,5},{5,4},{6,7},{7,6},{8,9},{9,8},{10,11... | collective-permute-start | bytes 147464 | tf_op jit(solution)/shard_map/ppermute | solution.py:24
  19.0 5.0 %collective-permute-start.16 = (bf16[408,128]{1,0:T(8,128)(2,1)S(1)}, bf16[408,128]{1,0:T(8,128)(2,1)S(1)}, u32[]{:S(2)}, u32[]{:S(2)}) collective-permute-start(bf16[408,128]{1,0:T(8,128)(2,1)S(1)} %attend.1.refs_0_), channel_id=1, source_target_pairs={{0,2},{1,3},{2,0},{3,1},{4,6},{5,7},{6,4},{7,5},{8,10},{9,11},{10,... | collective-permute-start | bytes 313352 | tf_op jit(solution)/shard_map/ppermute | solution.py:24
  20.6 3.5 %collective-permute-start.15 = (bf16[408,128]{1,0:T(8,128)(2,1)S(1)}, bf16[408,128]{1,0:T(8,128)(2,1)S(1)}, u32[]{:S(2)}, u32[]{:S(2)}) collective-permute-start(bf16[408,128]{1,0:T(8,128)(2,1)S(1)} %attend.1.refs_0_), channel_id=1, source_target_pairs={{0,1},{1,0},{2,3},{3,2},{4,5},{5,4},{6,7},{7,6},{8,9},{9,8},{10,11... | collective-permute-start | bytes 313352 | tf_op jit(solution)/shard_map/ppermute | solution.py:24
  24.0 1.3 %collective-permute-start.17 = (bf16[408,128]{1,0:T(8,128)(2,1)S(1)}, bf16[408,128]{1,0:T(8,128)(2,1)S(1)}, u32[]{:S(2)}, u32[]{:S(2)}) collective-permute-start(bf16[408,128]{1,0:T(8,128)(2,1)S(1)} %collective-permute-done.16.refs_2_), channel_id=1, source_target_pairs={{0,1},{1,0},{2,3},{3,2},{4,5},{5,4},{6,7},{7,6},{8,9},{9,8},{10,11... | collective-permute-start | bytes 313352 | tf_op jit(solution)/shard_map/ppermute | solution.py:24
  26.4 7.8 %collective-permute-start.18 = (bf16[208,128]{1,0:T(8,128)(2,1)S(1)}, bf16[208,128]{1,0:T(8,128)(2,1)S(1)}, u32[]{:S(2)}, u32[]{:S(2)}) collective-permute-start(bf16[208,128]{1,0:T(8,128)(2,1)S(1)} %get-tuple-element.10), channel_id=1, source_target_pairs={{0,8},{1,9},{2,10},{3,11},{4,12},{5,13},{6,14},{7,15},{8,0},{9,1},... | collective-permute-start | bytes 159752 | tf_op jit(solution)/shard_map/ppermute | solution.py:24
  27.9 6.3 %collective-permute-start.19 = (bf16[208,128]{1,0:T(8,128)(2,1)S(1)}, bf16[208,128]{1,0:T(8,128)(2,1)S(1)}, u32[]{:S(2)}, u32[]{:S(2)}) collective-permute-start(bf16[208,128]{1,0:T(8,128)(2,1)S(1)} %get-tuple-element.11), channel_id=1, source_target_pairs={{0,12},{1,13},{2,14},{3,15},{4,8},{5,9},{6,10},{7,11},{8,4},{9,5},... | collective-permute-start | bytes 159752 | tf_op jit(solution)/shard_map/ppermute | solution.py:24
  30.0 4.9 %collective-permute-start.20 = (bf16[208,128]{1,0:T(8,128)(2,1)S(1)}, bf16[208,128]{1,0:T(8,128)(2,1)S(1)}, u32[]{:S(2)}, u32[]{:S(2)}) collective-permute-start(bf16[208,128]{1,0:T(8,128)(2,1)S(1)} %get-tuple-element.12), channel_id=1, source_target_pairs={{0,4},{1,5},{2,6},{3,7},{4,0},{5,1},{6,2},{7,3},{8,12},{9,13},{10,... | collective-permute-start | bytes 159752 | tf_op jit(solution)/shard_map/ppermute | solution.py:24
